TPU v7x, 32 devices: a whole 2x2x4 slice. The times are simulated.
32 devices in a mesh: cp: 32 (over z, y, x, core).
Axes of the slice: x: 2, y: 2, z: 4, core: 2. Of those that a mesh axis runs over, the one named last changes fastest.
Arguments:
- queries: bfloat16 [16384, 512], P('cp'), may hold values from -6 to 6
- keys: bfloat16 [16384, 128], P('cp'), may hold values from -6 to 6
- values: bfloat16 [16384, 128], P('cp'), may hold values from -6 to 6
- grad_out: bfloat16 [16384, 512], P('cp'), may hold values from -6 to 6
- selections: int32 [32, 2], P('cp'), may hold values from -1 to 30, as said below
Outputs:
- attended: bfloat16 [16384, 512], P('cp')
- grad_queries: bfloat16 [16384, 512], P('cp')
- grad_keys: bfloat16 [16384, 128], P('cp')
- grad_values: bfloat16 [16384, 128], P('cp')
Inputs may be any that keep to these rules, and one draw needn't show every extreme that they name: `selections`: row b names two different blocks before block b; where block b has fewer than two earlier blocks, the missing entries are -1 (blocks 0 and 1 only).
All inputs are finite; a program needn't handle non-finite values.
Results may differ from a plain program's by a relative error of at most 0.015.
Values may be sent and summed in bfloat16 or wider, within the bound.
No kernel may reach another device: no remote copies, remote signals or barrier semaphores. Data moves between devices by JAX's collectives and lax.ppermute only.
A program may use at most 128 MiB of HBM per device.

v0:
```python
import jax
import jax.numpy as jnp
from jax import lax
from jax.sharding import PartitionSpec as P

HEADS = 4
HEAD_DIM = 128
BLK = 512
masked_value = -1e30


def key_mask(chosen):
    rows_at = lax.broadcasted_iota(jnp.int32, (BLK, BLK), 0)
    cols_at = lax.broadcasted_iota(jnp.int32, (BLK, BLK), 1)
    causal = cols_at <= rows_at
    first_ok = jnp.broadcast_to(chosen[0] >= 0, (BLK, BLK))
    second_ok = jnp.broadcast_to(chosen[1] >= 0, (BLK, BLK))
    return jnp.concatenate([causal, first_ok, second_ok], axis=1)


def attend_forward(query_rows, block_keys, allowed):
    score_scale = HEAD_DIM ** (-0.5)
    query_heads = query_rows.reshape(BLK, HEADS, HEAD_DIM)
    scores = (
        jnp.einsum("qhd,kd->hqk", query_heads, block_keys, preferred_element_type=jnp.float32)
        * score_scale
    )
    scores = jnp.where(allowed[None], scores, masked_value)
    row_max = jnp.max(scores, axis=-1, keepdims=True)
    exponent = jnp.exp(scores - row_max)
    weights = exponent / jnp.sum(exponent, axis=-1, keepdims=True)
    return (query_heads, weights, weights.astype(jnp.bfloat16))


def body(queries, keys, values, grad_out, selections):
    devices = lax.axis_size("cp")
    local_rows = queries.shape[0]
    local_blocks = local_rows // BLK
    piece_rows = BLK // devices
    head_width = keys.shape[1]
    pair_width = 2 * head_width
    score_scale = HEAD_DIM ** (-0.5)
    requests = lax.all_gather(selections, "cp", axis=0, tiled=True)
    local_pairs = jnp.concatenate([keys, values], axis=1)

    def block_inputs(member, gathered):
        joined = jnp.concatenate(
            [local_pairs, gathered[2 * member], gathered[2 * member + 1]], axis=0
        )
        return (joined[:, :head_width], joined[:, head_width:], key_mask(selections[member]))

    spread = lax.all_to_all(
        local_pairs.reshape(local_blocks, devices, piece_rows, pair_width),
        "cp",
        split_axis=1,
        concat_axis=0,
        tiled=True,
    )
    held_pieces = spread.reshape(local_blocks * devices, piece_rows, pair_width)
    wanted = jnp.maximum(requests, 0)
    outgoing = held_pieces[wanted]
    arrived = lax.all_to_all(outgoing, "cp", split_axis=0, concat_axis=2, tiled=True)
    fetched = arrived.reshape(2 * local_blocks, BLK, pair_width)
    member = 0
    block_keys, block_values, allowed = block_inputs(member, fetched)
    query_heads, weights, probs_low = attend_forward(queries, block_keys, allowed)
    output_heads = jnp.einsum(
        "hqk,kd->qhd", probs_low, block_values, preferred_element_type=jnp.float32
    )
    attended = output_heads.astype(jnp.bfloat16).reshape(BLK, HEADS * HEAD_DIM)
    slot_grads = []
    member = 0
    block_keys, block_values, allowed = block_inputs(member, fetched)
    query_heads, weights, probs_low = attend_forward(queries, block_keys, allowed)
    grad_heads = grad_out.reshape(BLK, HEADS, HEAD_DIM)
    grad_probs = jnp.einsum(
        "qhd,kd->hqk", grad_heads, block_values, preferred_element_type=jnp.float32
    )
    inner_sum = jnp.sum(weights * grad_probs, axis=-1, keepdims=True)
    grad_scores = (weights * (grad_probs - inner_sum)).astype(jnp.bfloat16)
    grad_query = (
        jnp.einsum("hqk,kd->qhd", grad_scores, block_keys, preferred_element_type=jnp.float32)
        * score_scale
    )
    grad_queries = grad_query.astype(jnp.bfloat16).reshape(BLK, HEADS * HEAD_DIM)
    grad_k = (
        jnp.einsum("hqk,qhd->kd", grad_scores, query_heads, preferred_element_type=jnp.float32)
        * score_scale
    )
    grad_v = jnp.einsum("hqk,qhd->kd", probs_low, grad_heads, preferred_element_type=jnp.float32)
    grad_both = jnp.concatenate([grad_k, grad_v], axis=1)
    own_grads = grad_both[:BLK]
    slot_grads.append(grad_both[BLK : 2 * BLK])
    slot_grads.append(grad_both[2 * BLK :])
    partials = jnp.stack(slot_grads).reshape(2 * local_blocks, devices, piece_rows, pair_width)
    received = lax.all_to_all(
        partials.astype(jnp.bfloat16), "cp", split_axis=1, concat_axis=1, tiled=True
    ).astype(partials.dtype)
    owners_ids = requests.T.reshape(-1)
    total_blocks = devices * local_blocks
    onehot = (owners_ids[None, :] == jnp.arange(total_blocks, dtype=jnp.int32)[:, None]).astype(
        jnp.float32
    )
    summed = jnp.dot(
        onehot,
        received.reshape(2 * local_blocks * devices, piece_rows * pair_width),
        precision=lax.Precision.HIGHEST,
    )
    returned = lax.all_to_all(
        summed.reshape(devices, local_blocks, piece_rows, pair_width).astype(jnp.bfloat16),
        "cp",
        split_axis=0,
        concat_axis=2,
        tiled=True,
    ).astype(jnp.float32)
    grad_pairs = returned.reshape(local_rows, pair_width) + own_grads
    return (
        attended,
        grad_queries,
        grad_pairs[:, :head_width].astype(jnp.bfloat16),
        grad_pairs[:, head_width:].astype(jnp.bfloat16),
    )


def solution(mesh):
    in_specs = (P("cp", None), P("cp", None), P("cp", None), P("cp", None), P("cp", None))
    out_specs = (P("cp", None), P("cp", None), P("cp", None), P("cp", None))
    return jax.shard_map(body, mesh=mesh, in_specs=in_specs, out_specs=out_specs, check_vma=False)
```

profile of v0, /device:TPU:0, one launch (start us, length us, event | category | flops | bytes accessed | tf_op | source)
XLA Modules:
  0.0 151.7 jit_solution(15815537463073276769)
XLA Ops:
  0.6 1.6 %constant_dynamic-update-slice_fusion.1 = bf16[512,256]{1,0:T(8,128)(2,1)} fusion(bf16[512,128]{1,0:T(8,128)(2,1)} %param.6), kind=kLoop, calls=%fused_computation.49 | loop fusion | bytes 262144
  2.2 1.6 %constant_dynamic-update-slice_fusion = bf16[512,256]{1,0:T(8,128)(2,1)} fusion(bf16[512,256]{1,0:T(8,128)(2,1)} %constant_dynamic-update-slice_fusion.1, bf16[512,128]{1,0:T(8,128)(2,1)} %param.7), kind=kLoop, calls=%fused_computation.48 | loop fusion | bytes 262144 | tf_op jit(solution)/shard_map/concatenate | solution.py:44
  3.8 7.3 %all-to-all-start = ((bf16[1,32,16,256]{3,2,0,1:T(8,128)(2,1)}), bf16[1,32,16,256]{3,2,0,1:T(8,128)(2,1)S(1)}, u32[]{:S(2)}, u32[]{:S(2)}) async-start(bf16[1,32,16,256]{3,2,0,1:T(8,128)(2,1)} %bitcast.1), calls=%async_computation | async-start | bytes 524288 | tf_op jit(solution)/shard_map/all_to_all | solution.py:52
  11.1 42.0 %all-gather = s32[32,1,2]{2,1,0:T(1,128)S(1)} all-gather(s32[1,1,2]{2,1,0:T(1,128)} %bitcast.108), channel_id=1, replica_groups=mesh['cp'=32] {'cp'}, dimensions={0}, use_global_device_ids=true | all-gather | bytes 264 | tf_op jit(solution)/shard_map/all_gather | solution.py:43
  53.4 1.4 gather_fusion
  54.8 2.6 %all-to-all-start.1 = ((bf16[32,2,16,256]{3,2,1,0:T(8,128)(2,1)}), bf16[32,2,16,256]{3,2,1,0:T(8,128)(2,1)S(1)}, u32[]{:S(2)}, u32[]{:S(2)}) async-start(bf16[32,2,16,256]{3,2,1,0:T(8,128)(2,1)} %bitcast.5), calls=%async_computation.1 | async-start | bytes 1048576 | tf_op jit(solution)/shard_map/all_to_all | solution.py:62
  57.4 1.3 copy.80
  58.6 1.3 fusion.37
  61.3 1.3 copy.81
  62.7 2.2 %add_add_fusion = pred[512,1536]{0,1:T(8,128)(4,1)} fusion(pred[512,512]{0,1:T(8,128)(4,1)S(1)} %iota_compare_fusion, pred[1536]{0:T(1024)(128)(4,1)S(1)} %pad.6.clone, pred[1536]{0:T(1024)(128)(4,1)S(1)} %pad.5.clone), kind=kLoop, calls=%fused_computation.18 | loop fusion | flops 1572864 | bytes 1051648 | tf_op jit(solution)/shard_map/concatenate | solution.py:18
  64.9 8.1 %all-to-all-done.1 = bf16[32,2,16,256]{3,2,1,0:T(8,128)(2,1)S(1)} async-done(((bf16[32,2,16,256]{3,2,1,0:T(8,128)(2,1)}), bf16[32,2,16,256]{3,2,1,0:T(8,128)(2,1)S(1)}, u32[]{:S(2)}, u32[]{:S(2)}) %all-to-all-start.1) | async-done | bytes 524320 | tf_op jit(solution)/shard_map/all_to_all | solution.py:62
  74.0 6.3 %fusion.28 = f32[1536,512,4]{1,0,2:T(8,128)} fusion(bf16[512,4,128]{0,2,1:T(8,128)(2,1)S(1)} %bitcast.96, bf16[1536,256]{1,0:T(8,128)(2,1)S(1)} %pad_maximum_fusion.1), kind=kOutput, calls=%fused_computation.42 | convolution fusion | flops 805306368 | bytes 13500416 | tf_op jit(solution)/shard_map/qhd,kd->hqk/dot_general | solution.py:25
  80.3 11.7 %fusion.38 = (f32[4,512]{1,0:T(4,128)S(1)}, f32[4,512,1536]{1,2,0:T(8,128)S(1)}) fusion(f32[1536,512,4]{1,0,2:T(8,128)} %fusion.28, pred[512,1536]{0,1:T(8,128)(4,1)} %add_add_fusion), kind=kOutput, calls=%fused_computation.57 | output fusion | flops 18875904 | bytes 25960448 | tf_op jit(solution)/shard_map/sub | solution.py:30
  92.0 5.9 %fusion.1 = (f32[4,512]{1,0:T(4,128)S(1)}, f32[1536,512,4]{1,0,2:T(8,128)}) fusion(f32[4,512,1536]{1,2,0:T(8,128)S(1)} %get-tuple-element.25, f32[4,512]{1,0:T(4,128)S(1)} %get-tuple-element.24, bf16[512,4,128]{0,2,1:T(8,128)(2,1)S(1)} %bitcast.105, bf16[1536,256]{1,0:T(8,128)(2,1)S(1)} %pad_maximum_fusion.1), kind=kOutput, calls=%fused_computation.4 | convolution fusion | flops 814741504 | bytes 26099712 | tf_op jit(solution)/shard_map/qhd,kd->hqk/dot_general | solution.py:76
  98.0 2.2 %fusion.12 = f32[1536,128]{0,1:T(8,128)S(1)} fusion(bf16[512,4,128]{0,2,1:T(8,128)(2,1)S(1)} %bitcast.106, f32[4,512,1536]{1,2,0:T(8,128)S(1)} %get-tuple-element.25, f32[4,512]{1,0:T(4,128)S(1)} %get-tuple-element.24), kind=kOutput, calls=%fused_computation.19 | convolution fusion | flops 811597824 | bytes 13901824 | tf_op jit(solution)/shard_map/hqk,qhd->kd/dot_general | solution.py:90
  100.3 6.8 %fusion.3 = bf16[4,512,1536]{1,2,0:T(8,128)(2,1)S(1)} fusion(f32[1536,512,4]{1,0,2:T(8,128)} %get-tuple-element.27, f32[4,512]{1,0:T(4,128)S(1)} %get-tuple-element.26, f32[4,512,1536]{1,2,0:T(8,128)S(1)} %get-tuple-element.25, f32[4,512]{1,0:T(4,128)S(1)} %get-tuple-element.24), kind=kLoop, calls=%fused_computation.6 | loop fusion | flops 12582912 | bytes 31473664 | tf_op jit(solution)/shard_map/convert_element_type | solution.py:80
  107.2 2.6 %copy-done = bf16[4,512,1536]{1,2,0:T(8,128)(2,1)} copy-done((bf16[4,512,1536]{1,2,0:T(8,128)(2,1)}, bf16[4,512,1536]{1,2,0:T(8,128)(2,1)S(1)}, u32[]{:S(2)}) %copy-start) | copy-done | bytes 6291480
  109.7 2.1 %fusion.15 = f32[1536,128]{0,1:T(8,128)S(1)} fusion(bf16[4,512,1536]{1,2,0:T(8,128)(2,1)S(1)} %fusion.3, bf16[512,4,128]{0,2,1:T(8,128)(2,1)S(1)} %bitcast.97), kind=kOutput, calls=%fused_computation.21 | convolution fusion | flops 805502976 | bytes 7602176 | tf_op jit(solution)/shard_map/hqk,qhd->kd/dot_general | solution.py:87
  114.0 2.9 %all-to-all-start.2 = ((bf16[2,32,16,256]{3,2,0,1:T(8,128)(2,1)}), bf16[2,32,16,256]{3,2,0,1:T(8,128)(2,1)S(1)}, u32[]{:S(2)}, u32[]{:S(2)}) async-start(bf16[2,32,16,256]{3,2,0,1:T(8,128)(2,1)} %copy.62), calls=%async_computation.2 | async-start | bytes 1048576 | tf_op jit(solution)/shard_map/all_to_all | solution.py:96
  117.0 15.5 %all-to-all-done.2 = bf16[2,32,16,256]{3,2,0,1:T(8,128)(2,1)S(1)} async-done(((bf16[2,32,16,256]{3,2,0,1:T(8,128)(2,1)}), bf16[2,32,16,256]{3,2,0,1:T(8,128)(2,1)S(1)}, u32[]{:S(2)}, u32[]{:S(2)}) %all-to-all-start.2) | async-done | bytes 524320 | tf_op jit(solution)/shard_map/all_to_all | solution.py:96
  133.7 3.5 %all-to-all-start.3 = ((bf16[32,1,16,256]{3,2,1,0:T(8,128)(2,1)}), bf16[32,1,16,256]{3,2,1,0:T(8,128)(2,1)}, u32[]{:S(2)}, u32[]{:S(2)}) async-start(bf16[32,1,16,256]{3,2,1,0:T(8,128)(2,1)} %copy.65), calls=%async_computation.3 | async-start | bytes 524288 | tf_op jit(solution)/shard_map/all_to_all | solution.py:109
  137.2 6.5 %fusion.18 = bf16[128,4,512]{2,0,1:T(8,128)(2,1)} fusion(bf16[1536,256]{1,0:T(8,128)(2,1)S(1)} %pad_maximum_fusion.1, f32[4,512,1536]{1,2,0:T(8,128)} %copy-done.1, f32[4,512]{1,0:T(4,128)S(1)} %get-tuple-element.24), kind=kOutput, calls=%fused_computation.28 | convolution fusion | flops 811859968 | bytes 13508608 | tf_op jit(solution)/shard_map/hqk,kd->qhd/dot_general | solution.py:67
  145.8 2.0 %copy.68 = bf16[512,512]{1,0:T(8,128)(2,1)} copy(bf16[512,512]{0,1:T(8,128)(2,1)} %bitcast.107) | data formatting | bytes 1048576
  149.0 1.1 fusion.24
  (43 shorter events, 9.7 us)
Async XLA Ops:
  3.8 49.6 %all-to-all-start = ((bf16[1,32,16,256]{3,2,0,1:T(8,128)(2,1)}), bf16[1,32,16,256]{3,2,0,1:T(8,128)(2,1)S(1)}, u32[]{:S(2)}, u32[]{:S(2)}) async-start(bf16[1,32,16,256]{3,2,0,1:T(8,128)(2,1)} %bitcast.1), calls=%async_computation | async-start | bytes 524288 | tf_op jit(solution)/shard_map/all_to_all | solution.py:52
  54.8 18.2 %all-to-all-start.1 = ((bf16[32,2,16,256]{3,2,1,0:T(8,128)(2,1)}), bf16[32,2,16,256]{3,2,1,0:T(8,128)(2,1)S(1)}, u32[]{:S(2)}, u32[]{:S(2)}) async-start(bf16[32,2,16,256]{3,2,1,0:T(8,128)(2,1)} %bitcast.5), calls=%async_computation.1 | async-start | bytes 1048576 | tf_op jit(solution)/shard_map/all_to_all | solution.py:62
  92.0 8.3 %copy-start.1 = (f32[4,512,1536]{1,2,0:T(8,128)}, f32[4,512,1536]{1,2,0:T(8,128)S(1)}, u32[]{:S(2)}) copy-start(f32[4,512,1536]{1,2,0:T(8,128)S(1)} %get-tuple-element.25) | copy-start | bytes 37748740
  100.2 11.7 %copy-start.2 = (f32[1536,128]{0,1:T(8,128)}, f32[1536,128]{0,1:T(8,128)S(1)}, u32[]{:S(2)}) copy-start(f32[1536,128]{0,1:T(8,128)S(1)} %fusion.12) | copy-start | bytes 2359300
  107.2 2.6 %copy-start = (bf16[4,512,1536]{1,2,0:T(8,128)(2,1)}, bf16[4,512,1536]{1,2,0:T(8,128)(2,1)S(1)}, u32[]{:S(2)}) copy-start(bf16[4,512,1536]{1,2,0:T(8,128)(2,1)S(1)} %fusion.3) | copy-start | bytes 18874372
  111.9 0.9 copy-start.3
  114.0 18.5 %all-to-all-start.2 = ((bf16[2,32,16,256]{3,2,0,1:T(8,128)(2,1)}), bf16[2,32,16,256]{3,2,0,1:T(8,128)(2,1)S(1)}, u32[]{:S(2)}, u32[]{:S(2)}) async-start(bf16[2,32,16,256]{3,2,0,1:T(8,128)(2,1)} %copy.62), calls=%async_computation.2 | async-start | bytes 1048576 | tf_op jit(solution)/shard_map/all_to_all | solution.py:96
  132.8 10.9 %slice-start = ((s8[6291456]{0:T(1024)(128)(4,1)}), s8[2097152]{0:T(1024)(128)(4,1)S(1)}, s32[]{:S(2)}) async-start(s8[6291456]{0:T(1024)(128)(4,1)} %bitcast.93), calls=%async_computation.4 | async-start | bytes 4194304
  133.7 14.1 %all-to-all-start.3 = ((bf16[32,1,16,256]{3,2,1,0:T(8,128)(2,1)}), bf16[32,1,16,256]{3,2,1,0:T(8,128)(2,1)}, u32[]{:S(2)}, u32[]{:S(2)}) async-start(bf16[32,1,16,256]{3,2,1,0:T(8,128)(2,1)} %copy.65), calls=%async_computation.3 | async-start | bytes 524288 | tf_op jit(solution)/shard_map/all_to_all | solution.py:109
  137.2 6.5 %slice-start.1 = ((s8[6291456]{0:T(1024)(128)(4,1)}), s8[4194304]{0:T(1024)(128)(4,1)S(1)}, s32[]{:S(2)}) async-start(s8[6291456]{0:T(1024)(128)(4,1)} %bitcast.93), calls=%async_computation.5 | async-start | bytes 8388608
where the time goes:
time: 152 us
  blocking collectives  42 us (28%)
  matrix products  24.4 us (16%)
  other arithmetic  24 us (16%)
  waiting for transfers between devices  23.6 us (16%)
  local copies, waits for them, and re-layouts  19.1 us (13%)
  starting transfers between devices  16.3 us (11%)
  between operations  2.2 us (1%)
    all_gather x1, blocking collectives, body(): requests = lax.all_gather(selections, 'cp', axis=0, tiled=True)  42 us
    all_to_all x1, waiting for transfers between devices, body(): lax.all_to_all(partials.astype(jnp.bfloat16), 'cp', split_axis=1, concat_...  15.5 us
    sub x1, other arithmetic, attend_forward(): exponent = jnp.exp(scores - row_max)  11.7 us
    unnamed x17, local copies, waits for them, and re-layouts  9.67 us
    all_to_all x1, waiting for transfers between devices, body(): lax.all_to_all(outgoing, 'cp', split_axis=0, concat_axis=2, tiled=True)  8.1 us
    all_to_all x1, starting transfers between devices, body(): lax.all_to_all(local_pairs.reshape(local_blocks, devices, piece_rows, pai...  7.33 us
    convert_element_type x1, other arithmetic, body(): grad_scores = (weights * (grad_probs - inner_sum)).astype(jnp.bfloat16)  6.82 us
    dot_general x1, matrix products, body(): jnp.einsum('hqk,kd->qhd', probs_low, block_values, preferred_element_type...  6.53 us
  transfers between devices with their start and end apart: 4, of which 2 were waited for; matrix products, arithmetic and copies ran while one was open for 11% of the time, Pallas kernels for 0%

commit v1 on v0

--- a/solution.py
+++ b/solution.py
@@ -59,7 +59,10 @@
     held_pieces = spread.reshape(local_blocks * devices, piece_rows, pair_width)
     wanted = jnp.maximum(requests, 0)
     outgoing = held_pieces[wanted]
-    arrived = lax.all_to_all(outgoing, "cp", split_axis=0, concat_axis=2, tiled=True)
+    arrived = jnp.concatenate(
+        lax.all_to_all(jnp.stack(jnp.split(outgoing, lax.axis_size("cp"), axis=0)), "cp", 0, 0),
+        axis=2,
+    )
     fetched = arrived.reshape(2 * local_blocks, BLK, pair_width)
     member = 0
     block_keys, block_values, allowed = block_inputs(member, fetched)

time: 152 us -> 171 us (1.12)
  local copies, waits for them, and re-layouts: 19.1 us -> 37.6 us
    unnamed x17 -> x48, local copies, waits for them, and re-layouts: 9.67 us -> 28.3 us
  transfers between devices with their start and end apart: 4 -> 4, of which waited for: 2 -> 2; matrix products, arithmetic and copies ran while one was open for 11% -> 10% of each run, Pallas kernels for 0% -> 0%
where the time goes in v1:
time: 171 us; the launch traced here: 170 us
  blocking collectives  42 us (25%)
  local copies, waits for them, and re-layouts  37.6 us (22%)
  matrix products  24.6 us (14%)
  other arithmetic  23.9 us (14%)
  waiting for transfers between devices  23.6 us (14%)
  starting transfers between devices  16.3 us (10%)
  between operations  2.22 us (1%)
    all_gather x1, blocking collectives, body(): requests = lax.all_gather(selections, 'cp', axis=0, tiled=True)  42 us
    unnamed x48, local copies, waits for them, and re-layouts  28.3 us
    all_to_all x1, waiting for transfers between devices, body(): lax.all_to_all(partials.astype(jnp.bfloat16), 'cp', split_axis=1, concat_...  15.5 us
    sub x1, other arithmetic, attend_forward(): exponent = jnp.exp(scores - row_max)  11.7 us
    all_to_all x1, waiting for transfers between devices, body(): lax.all_to_all(jnp.stack(jnp.split(outgoing, lax.axis_size('cp'), axis=0)...  8.1 us
    all_to_all x1, starting transfers between devices, body(): lax.all_to_all(local_pairs.reshape(local_blocks, devices, piece_rows, pai...  7.33 us
    convert_element_type x1, other arithmetic, body(): grad_scores = (weights * (grad_probs - inner_sum)).astype(jnp.bfloat16)  6.69 us
    dot_general x1, matrix products, body(): jnp.einsum('hqk,kd->qhd', probs_low, block_values, preferred_element_type...  6.53 us
  transfers between devices with their start and end apart: 4, of which 2 were waited for; matrix products, arithmetic and copies ran while one was open for 10% of the time, Pallas kernels for 0%

profile of v1, /device:TPU:0, one launch (start us, length us, event | category | flops | bytes accessed | tf_op | source)
XLA Modules:
  0.0 170.2 jit_solution(15794489548778190725)
XLA Ops:
  0.6 1.6 constant_dynamic-update-slice_fusion.1
  2.2 1.6 constant_dynamic-update-slice_fusion
  3.8 7.3 %all-to-all-start = ((bf16[1,32,16,256]{3,2,0,1:T(8,128)(2,1)}), bf16[1,32,16,256]{3,2,0,1:T(8,128)(2,1)S(1)}, u32[]{:S(2)}, u32[]{:S(2)}) async-start(bf16[1,32,16,256]{3,2,0,1:T(8,128)(2,1)} %bitcast.1), calls=%async_computation | async-start | bytes 524288 | tf_op jit(solution)/shard_map/all_to_all | solution.py:52
  11.1 42.0 %all-gather = s32[32,1,2]{2,1,0:T(1,128)S(1)} all-gather(s32[1,1,2]{2,1,0:T(1,128)} %bitcast.233), channel_id=1, replica_groups=mesh['cp'=32] {'cp'}, dimensions={0}, use_global_device_ids=true | all-gather | bytes 264 | tf_op jit(solution)/shard_map/all_gather | solution.py:43
  73.4 2.6 %all-to-all-start.1 = ((bf16[32,1,2,16,256]{4,3,2,1,0:T(8,128)(2,1)}), bf16[32,1,2,16,256]{4,3,2,1,0:T(8,128)(2,1)S(1)}, u32[]{:S(2)}, u32[]{:S(2)}) async-start(bf16[32,1,2,16,256]{4,3,2,1,0:T(8,128)(2,1)} %constant_dynamic-update-slice_fusion.2), calls=%async_computation.1 | async-start | bytes 1048576 | tf_op jit(solution)/shard_map/all_to_all | solution.py:63
  76.0 1.3 copy.142
  77.3 1.3 fusion.37
  79.9 1.3 copy.143
  81.3 2.2 %add_add_fusion = pred[512,1536]{0,1:T(8,128)(4,1)} fusion(pred[512,512]{0,1:T(8,128)(4,1)S(1)} %iota_compare_fusion, pred[1536]{0:T(1024)(128)(4,1)S(1)} %pad.6.clone, pred[1536]{0:T(1024)(128)(4,1)S(1)} %pad.5.clone), kind=kLoop, calls=%fused_computation.18 | loop fusion | flops 1572864 | bytes 1051648 | tf_op jit(solution)/shard_map/concatenate | solution.py:18
  83.5 8.1 %all-to-all-done.1 = bf16[32,1,2,16,256]{4,3,2,1,0:T(8,128)(2,1)S(1)} async-done(((bf16[32,1,2,16,256]{4,3,2,1,0:T(8,128)(2,1)}), bf16[32,1,2,16,256]{4,3,2,1,0:T(8,128)(2,1)S(1)}, u32[]{:S(2)}, u32[]{:S(2)}) %all-to-all-start.1) | async-done | bytes 524320 | tf_op jit(solution)/shard_map/all_to_all | solution.py:63
  92.7 6.3 %fusion.28 = f32[1536,512,4]{1,0,2:T(8,128)} fusion(bf16[512,4,128]{0,2,1:T(8,128)(2,1)S(1)} %bitcast.221, bf16[1536,256]{1,0:T(8,128)(2,1)S(1)} %pad_maximum_fusion.1), kind=kOutput, calls=%fused_computation.42 | convolution fusion | flops 805306368 | bytes 13500416 | tf_op jit(solution)/shard_map/qhd,kd->hqk/dot_general | solution.py:25
  99.0 11.7 %fusion.38 = (f32[4,512]{1,0:T(4,128)S(1)}, f32[4,512,1536]{1,2,0:T(8,128)S(1)}) fusion(f32[1536,512,4]{1,0,2:T(8,128)} %fusion.28, pred[512,1536]{0,1:T(8,128)(4,1)} %add_add_fusion), kind=kOutput, calls=%fused_computation.121 | output fusion | flops 18875904 | bytes 25960448 | tf_op jit(solution)/shard_map/sub | solution.py:30
  110.7 2.2 %fusion.12 = f32[1536,128]{0,1:T(8,128)S(1)} fusion(bf16[512,4,128]{0,2,1:T(8,128)(2,1)S(1)} %bitcast.230, f32[4,512,1536]{1,2,0:T(8,128)S(1)} %get-tuple-element.25, f32[4,512]{1,0:T(4,128)S(1)} %get-tuple-element.24), kind=kOutput, calls=%fused_computation.19 | convolution fusion | flops 811597824 | bytes 13901824 | tf_op jit(solution)/shard_map/hqk,qhd->kd/dot_general | solution.py:93
  112.9 6.1 %fusion.1 = (f32[4,512]{1,0:T(4,128)S(1)}, f32[1536,512,4]{1,0,2:T(8,128)}) fusion(f32[4,512,1536]{1,2,0:T(8,128)S(1)} %get-tuple-element.25, f32[4,512]{1,0:T(4,128)S(1)} %get-tuple-element.24, bf16[512,4,128]{0,2,1:T(8,128)(2,1)S(1)} %bitcast.231, bf16[1536,256]{1,0:T(8,128)(2,1)S(1)} %pad_maximum_fusion.1), kind=kOutput, calls=%fused_computation.4 | convolution fusion | flops 814741504 | bytes 26099712 | tf_op jit(solution)/shard_map/qhd,kd->hqk/dot_general | solution.py:79
  119.0 6.7 %fusion.3 = bf16[4,512,1536]{1,2,0:T(8,128)(2,1)S(1)} fusion(f32[1536,512,4]{1,0,2:T(8,128)} %get-tuple-element.27, f32[4,512]{1,0:T(4,128)S(1)} %get-tuple-element.26, f32[4,512,1536]{1,2,0:T(8,128)S(1)} %get-tuple-element.25, f32[4,512]{1,0:T(4,128)S(1)} %get-tuple-element.24), kind=kLoop, calls=%fused_computation.6 | loop fusion | flops 12582912 | bytes 31473664 | tf_op jit(solution)/shard_map/convert_element_type | solution.py:83
  125.7 2.6 %copy-done = bf16[4,512,1536]{1,2,0:T(8,128)(2,1)} copy-done((bf16[4,512,1536]{1,2,0:T(8,128)(2,1)}, bf16[4,512,1536]{1,2,0:T(8,128)(2,1)S(1)}, u32[]{:S(2)}) %copy-start) | copy-done | bytes 6291480
  128.3 2.1 %fusion.15 = f32[1536,128]{0,1:T(8,128)S(1)} fusion(bf16[4,512,1536]{1,2,0:T(8,128)(2,1)S(1)} %fusion.3, bf16[512,4,128]{0,2,1:T(8,128)(2,1)S(1)} %bitcast.222), kind=kOutput, calls=%fused_computation.21 | convolution fusion | flops 805502976 | bytes 7602176 | tf_op jit(solution)/shard_map/hqk,qhd->kd/dot_general | solution.py:90
  132.5 2.9 %all-to-all-start.2 = ((bf16[2,32,16,256]{3,2,0,1:T(8,128)(2,1)}), bf16[2,32,16,256]{3,2,0,1:T(8,128)(2,1)S(1)}, u32[]{:S(2)}, u32[]{:S(2)}) async-start(bf16[2,32,16,256]{3,2,0,1:T(8,128)(2,1)} %copy.124), calls=%async_computation.2 | async-start | bytes 1048576 | tf_op jit(solution)/shard_map/all_to_all | solution.py:99
  135.5 15.5 %all-to-all-done.2 = bf16[2,32,16,256]{3,2,0,1:T(8,128)(2,1)S(1)} async-done(((bf16[2,32,16,256]{3,2,0,1:T(8,128)(2,1)}), bf16[2,32,16,256]{3,2,0,1:T(8,128)(2,1)S(1)}, u32[]{:S(2)}, u32[]{:S(2)}) %all-to-all-start.2) | async-done | bytes 524320 | tf_op jit(solution)/shard_map/all_to_all | solution.py:99
  152.2 3.5 %all-to-all-start.3 = ((bf16[32,1,16,256]{3,2,1,0:T(8,128)(2,1)}), bf16[32,1,16,256]{3,2,1,0:T(8,128)(2,1)}, u32[]{:S(2)}, u32[]{:S(2)}) async-start(bf16[32,1,16,256]{3,2,1,0:T(8,128)(2,1)} %copy.127), calls=%async_computation.3 | async-start | bytes 524288 | tf_op jit(solution)/shard_map/all_to_all | solution.py:112
  155.7 6.5 %fusion.18 = bf16[128,4,512]{2,0,1:T(8,128)(2,1)} fusion(bf16[1536,256]{1,0:T(8,128)(2,1)S(1)} %pad_maximum_fusion.1, f32[4,512,1536]{1,2,0:T(8,128)} %copy-done.1, f32[4,512]{1,0:T(4,128)S(1)} %get-tuple-element.24), kind=kOutput, calls=%fused_computation.28 | convolution fusion | flops 811859968 | bytes 13508608 | tf_op jit(solution)/shard_map/hqk,kd->qhd/dot_general | solution.py:70
  162.3 1.0 fusion.17
  164.3 2.0 %copy.130 = bf16[512,512]{1,0:T(8,128)(2,1)} copy(bf16[512,512]{0,1:T(8,128)(2,1)} %bitcast.232) | data formatting | bytes 1048576
  167.5 1.1 fusion.24
  (75 shorter events, 28.5 us)
Async XLA Ops:
  3.8 49.6 %all-to-all-start = ((bf16[1,32,16,256]{3,2,0,1:T(8,128)(2,1)}), bf16[1,32,16,256]{3,2,0,1:T(8,128)(2,1)S(1)}, u32[]{:S(2)}, u32[]{:S(2)}) async-start(bf16[1,32,16,256]{3,2,0,1:T(8,128)(2,1)} %bitcast.1), calls=%async_computation | async-start | bytes 524288 | tf_op jit(solution)/shard_map/all_to_all | solution.py:52
  73.4 18.2 %all-to-all-start.1 = ((bf16[32,1,2,16,256]{4,3,2,1,0:T(8,128)(2,1)}), bf16[32,1,2,16,256]{4,3,2,1,0:T(8,128)(2,1)S(1)}, u32[]{:S(2)}, u32[]{:S(2)}) async-start(bf16[32,1,2,16,256]{4,3,2,1,0:T(8,128)(2,1)} %constant_dynamic-update-slice_fusion.2), calls=%async_computation.1 | async-start | bytes 1048576 | tf_op jit(solution)/shard_map/all_to_all | solution.py:63
  110.6 8.3 %copy-start.1 = (f32[4,512,1536]{1,2,0:T(8,128)}, f32[4,512,1536]{1,2,0:T(8,128)S(1)}, u32[]{:S(2)}) copy-start(f32[4,512,1536]{1,2,0:T(8,128)S(1)} %get-tuple-element.25) | copy-start | bytes 37748740
  112.9 17.5 %copy-start.2 = (f32[1536,128]{0,1:T(8,128)}, f32[1536,128]{0,1:T(8,128)S(1)}, u32[]{:S(2)}) copy-start(f32[1536,128]{0,1:T(8,128)S(1)} %fusion.12) | copy-start | bytes 2359300
  125.7 2.6 %copy-start = (bf16[4,512,1536]{1,2,0:T(8,128)(2,1)}, bf16[4,512,1536]{1,2,0:T(8,128)(2,1)S(1)}, u32[]{:S(2)}) copy-start(bf16[4,512,1536]{1,2,0:T(8,128)(2,1)S(1)} %fusion.3) | copy-start | bytes 18874372
  130.4 0.9 copy-start.3
  132.5 18.5 %all-to-all-start.2 = ((bf16[2,32,16,256]{3,2,0,1:T(8,128)(2,1)}), bf16[2,32,16,256]{3,2,0,1:T(8,128)(2,1)S(1)}, u32[]{:S(2)}, u32[]{:S(2)}) async-start(bf16[2,32,16,256]{3,2,0,1:T(8,128)(2,1)} %copy.124), calls=%async_computation.2 | async-start | bytes 1048576 | tf_op jit(solution)/shard_map/all_to_all | solution.py:99
  151.3 10.9 %slice-start = ((s8[6291456]{0:T(1024)(128)(4,1)}), s8[2097152]{0:T(1024)(128)(4,1)S(1)}, s32[]{:S(2)}) async-start(s8[6291456]{0:T(1024)(128)(4,1)} %bitcast.218), calls=%async_computation.4 | async-start | bytes 4194304
  152.2 14.1 %all-to-all-start.3 = ((bf16[32,1,16,256]{3,2,1,0:T(8,128)(2,1)}), bf16[32,1,16,256]{3,2,1,0:T(8,128)(2,1)}, u32[]{:S(2)}, u32[]{:S(2)}) async-start(bf16[32,1,16,256]{3,2,1,0:T(8,128)(2,1)} %copy.127), calls=%async_computation.3 | async-start | bytes 524288 | tf_op jit(solution)/shard_map/all_to_all | solution.py:112
  155.7 6.5 %slice-start.1 = ((s8[6291456]{0:T(1024)(128)(4,1)}), s8[4194304]{0:T(1024)(128)(4,1)S(1)}, s32[]{:S(2)}) async-start(s8[6291456]{0:T(1024)(128)(4,1)} %bitcast.218), calls=%async_computation.5 | async-start | bytes 8388608
